TPU v7x, 32 devices: a whole 2x2x4 slice. The times are simulated.
32 devices in a mesh: dp: 4 (over y, core), mp: 8 (over z, x).
Axes of the slice: x: 2, y: 2, z: 4, core: 2. Of those that a mesh axis runs over, the one named last changes fastest.
Arguments:
- tokens: bfloat16 [9216, 1024], P(('dp', 'mp')), may hold values from -6 to 6
- image_ids: int32 [9216], P('dp'), may hold values from 0 to 1, as said below
- lengths: int32 [4, 2], P('dp'), may hold values from 0 to 2304, as said below
- w_qkv: bfloat16 [3, 1024, 1024], P(None, None, 'mp'), may hold values from -0.1875 to 0.1875
- bias_query: float32 [1024], P('mp'), may hold values from -3 to 3
- bias_value: float32 [1024], P('mp'), may hold values from -0.3 to 0.3
- w_out: bfloat16 [1024, 1024], P('mp'), may hold values from -3 to 3
- w_up: bfloat16 [1024, 4096], P(None, 'mp'), may hold values from -0.1875 to 0.1875
- bias_up: float32 [4096], P('mp'), may hold values from -3 to 3
- w_down: bfloat16 [4096, 1024], P('mp'), may hold values from -0.09375 to 0.09375
- out_biases: float32 [2, 1024], replicated, may hold values from -2 to 2
- norm_gain: float32 [2, 1024], replicated, may hold values from 0.25 to 1.75
- norm_bias: float32 [2, 1024], replicated, may hold values from -2 to 2
- cotangent: bfloat16 [9216, 1024], P(('dp', 'mp')), may hold values from -6 to 6
Outputs:
- output: bfloat16 [9216, 1024], P(('dp', 'mp'))
- input_grad: bfloat16 [9216, 1024], P(('dp', 'mp'))
- grad_w_qkv: float32 [3, 1024, 1024], P(None, None, 'mp')
- grad_bias_query: float32 [1024], P('mp')
- grad_bias_value: float32 [1024], P('mp')
- grad_w_out: float32 [1024, 1024], P('mp')
- grad_w_up: float32 [1024, 4096], P(None, 'mp')
- grad_bias_up: float32 [4096], P('mp')
- grad_w_down: float32 [4096, 1024], P('mp')
- grad_out_biases: float32 [2, 1024], replicated
- grad_norm_gain: float32 [2, 1024], replicated
- grad_norm_bias: float32 [2, 1024], replicated
Inputs may be any that keep to these rules, and one draw needn't show every extreme that they name: `image_ids`: within each group of 2304 rows (one group for each index of dp) the image numbers never fall: a group holds either one image over all its rows, or two images of 1152 rows each. lengths[g, k] counts the valid rows at the start of image k of group g: 2304 for an image that fills its group (the second entry is then 0), else 1024. Some group holds an image of 2304 rows.
All inputs are finite; a program needn't handle non-finite values.
Results may differ from a plain program's by a relative error of at most 0.02.
Values may be sent and summed in bfloat16 or wider, within the bound.
A program may use at most 128 MiB of HBM per device.

v0:
```python
import jax
import jax.numpy as jnp
from jax import lax
from jax.sharding import PartitionSpec as P

HEAD_DIM = 64
BLOCK = 768
epsilon = 1e-06


def layer_norm(values, gain_vec, shift_vec):
    row_mean = jnp.mean(values, axis=-1, keepdims=True)
    centered = values - row_mean
    variance = jnp.mean(centered * centered, axis=-1, keepdims=True)
    return centered * lax.rsqrt(variance + epsilon) * gain_vec + shift_vec


def exact_gelu(values):
    return jax.nn.gelu(values, approximate=False)


def valid_rows(image_ids, group_lengths):
    total_rows = image_ids.shape[0]
    row_index = jnp.arange(total_rows, dtype=jnp.int32)
    member = image_ids[:, None] == jnp.arange(2, dtype=jnp.int32)[None, :]
    first_row = jnp.min(jnp.where(member, row_index[:, None], total_rows), axis=0)
    row_start = jnp.sum(jnp.where(member, first_row[None, :], 0), axis=1)
    row_limit = jnp.sum(jnp.where(member, group_lengths[None, :], 0), axis=1)
    return row_index - row_start < row_limit


def allowed_keys(first_query, image_ids, valid_mask):
    total_rows = image_ids.shape[0]
    row_index = jnp.arange(total_rows, dtype=jnp.int32)
    query_rows = first_query + jnp.arange(BLOCK, dtype=jnp.int32)
    query_ids = lax.dynamic_slice_in_dim(image_ids, first_query, BLOCK, 0)
    same_image = (query_ids[:, None] == image_ids[None, :]) & valid_mask[None, :]
    return same_image | (query_rows[:, None] == row_index[None, :])


def block_scores(query_block, keys_all, first_query, image_ids, valid_mask):
    scores = jnp.einsum(
        "qhd,khd->hqk", query_block, keys_all, preferred_element_type=jnp.float32
    ) * HEAD_DIM ** (-0.5)
    allowed = allowed_keys(first_query, image_ids, valid_mask)
    return jnp.where(allowed[None, :, :], scores, -1e30)


def attend_forward(queries, keys_all, values_all, image_ids, valid_mask):

    def one_block(block_number):
        first_query = block_number * BLOCK
        query_block = lax.dynamic_slice_in_dim(queries, first_query, BLOCK, 0)
        scores = block_scores(query_block, keys_all, first_query, image_ids, valid_mask)
        row_max = jnp.max(scores, axis=-1)
        weights = jnp.exp(scores - row_max[:, :, None])
        row_total = jnp.sum(weights, axis=-1)
        probs_low = (weights / row_total[:, :, None]).astype(jnp.bfloat16)
        attended = jnp.einsum(
            "hqk,khd->qhd", probs_low, values_all, preferred_element_type=jnp.float32
        )
        return (attended.astype(jnp.bfloat16), row_max + jnp.log(row_total))

    block_count = queries.shape[0] // BLOCK
    attended, log_totals = lax.map(one_block, jnp.arange(block_count, dtype=jnp.int32))
    return (attended.reshape(queries.shape), log_totals)


def attend_backward(
    queries, keys_all, values_all, log_totals, grad_attended, image_ids, valid_mask
):
    scale_factor = HEAD_DIM ** (-0.5)
    block_count = queries.shape[0] // BLOCK

    def scan_step(totals, block_number):
        key_total, value_total = totals
        first_query = block_number * BLOCK
        query_block = lax.dynamic_slice_in_dim(queries, first_query, BLOCK, 0)
        grad_block = lax.dynamic_slice_in_dim(grad_attended, first_query, BLOCK, 0)
        scores = block_scores(query_block, keys_all, first_query, image_ids, valid_mask)
        probabilities = jnp.exp(scores - log_totals[block_number][:, :, None])
        probs_low = probabilities.astype(jnp.bfloat16)
        value_total = value_total + jnp.einsum(
            "hqk,qhd->khd", probs_low, grad_block, preferred_element_type=jnp.float32
        )
        grad_probs = jnp.einsum(
            "qhd,khd->hqk", grad_block, values_all, preferred_element_type=jnp.float32
        )
        inner_sum = jnp.sum(probabilities * grad_probs, axis=-1, keepdims=True)
        grad_scores = (probabilities * (grad_probs - inner_sum)).astype(jnp.bfloat16)
        grad_query = (
            jnp.einsum("hqk,khd->qhd", grad_scores, keys_all, preferred_element_type=jnp.float32)
            * scale_factor
        )
        key_total = (
            key_total
            + jnp.einsum(
                "hqk,qhd->khd", grad_scores, query_block, preferred_element_type=jnp.float32
            )
            * scale_factor
        )
        return ((key_total, value_total), grad_query.astype(jnp.bfloat16))

    zero_state = jnp.zeros(queries.shape, jnp.float32)
    (key_total, value_total), grad_queries = lax.scan(
        scan_step, (zero_state, zero_state), jnp.arange(block_count, dtype=jnp.int32)
    )
    return (
        grad_queries.reshape(queries.shape),
        key_total.astype(jnp.bfloat16),
        value_total.astype(jnp.bfloat16),
    )


def body(
    tokens,
    image_ids,
    lengths,
    w_qkv,
    bias_query,
    bias_value,
    w_out,
    w_up,
    bias_up,
    w_down,
    out_biases,
    norm_gain,
    norm_bias,
    cotangent,
):
    share_rows = tokens.shape[0]
    local_width = w_qkv.shape[2]
    local_heads = local_width // HEAD_DIM
    total_rows = image_ids.shape[0]
    model_index = lax.axis_index("mp")
    valid_mask = valid_rows(image_ids, lengths[0])
    own_valid = lax.dynamic_slice_in_dim(
        valid_mask.astype(jnp.float32), model_index * share_rows, share_rows, 0
    )

    def split_heads(matrix):
        return matrix.reshape(total_rows, local_heads, HEAD_DIM)

    inputs_f = tokens.astype(jnp.float32)
    normed_one = layer_norm(inputs_f, norm_gain[0], norm_bias[0]).astype(jnp.bfloat16)
    gathered_one = lax.all_gather(normed_one, "mp", axis=0, tiled=True)
    projected = jnp.einsum("rd,tde->tre", gathered_one, w_qkv, preferred_element_type=jnp.float32)
    queries = split_heads((projected[0] + bias_query).astype(jnp.bfloat16))
    keys_all = split_heads(projected[1].astype(jnp.bfloat16))
    values_all = split_heads((projected[2] + bias_value).astype(jnp.bfloat16))
    attended, log_totals = attend_forward(queries, keys_all, values_all, image_ids, valid_mask)
    attended = attended.reshape(total_rows, local_width)
    hidden_one = (
        inputs_f
        + lax.psum_scatter(
            jnp.dot(attended, w_out, preferred_element_type=jnp.float32).astype(jnp.bfloat16),
            "mp",
            scatter_dimension=0,
            tiled=True,
        ).astype(jnp.float32)
        + out_biases[0]
    )
    normed_two = layer_norm(hidden_one, norm_gain[1], norm_bias[1]).astype(jnp.bfloat16)
    gathered_two = lax.all_gather(normed_two, "mp", axis=0, tiled=True)
    pre_act = jnp.dot(gathered_two, w_up, preferred_element_type=jnp.float32) + bias_up
    activated = exact_gelu(pre_act).astype(jnp.bfloat16)
    output_full = (
        hidden_one
        + lax.psum_scatter(
            jnp.dot(activated, w_down, preferred_element_type=jnp.float32).astype(jnp.bfloat16),
            "mp",
            scatter_dimension=0,
            tiled=True,
        ).astype(jnp.float32)
        + out_biases[1]
    )
    kept_state = (
        gathered_one,
        queries,
        keys_all,
        values_all,
        log_totals,
        attended,
        hidden_one,
        gathered_two,
        pre_act,
        activated,
    )
    output_full, kept_state = (output_full, kept_state)
    (
        gathered_one,
        queries,
        keys_all,
        values_all,
        log_totals,
        attended,
        hidden_one,
        gathered_two,
        pre_act,
        activated,
    ) = kept_state
    tokens_f = tokens.astype(jnp.float32)
    grad_out = cotangent.astype(jnp.float32) * own_valid[:, None]
    grad_mlp = lax.all_gather(grad_out.astype(jnp.bfloat16), "mp", axis=0, tiled=True)
    grad_w_down = jnp.einsum("rf,rd->fd", activated, grad_mlp, preferred_element_type=jnp.float32)
    grad_act = jnp.einsum("rd,fd->rf", grad_mlp, w_down, preferred_element_type=jnp.float32)
    _, gelu_back = jax.vjp(exact_gelu, pre_act)
    grad_pre = gelu_back(grad_act)[0].astype(jnp.bfloat16)
    grad_w_up = jnp.einsum("rd,rf->df", gathered_two, grad_pre, preferred_element_type=jnp.float32)
    grad_bias_up = jnp.sum(grad_pre, axis=0, dtype=jnp.float32)
    grad_normed_two = lax.psum_scatter(
        jnp.einsum("rf,df->rd", grad_pre, w_up, preferred_element_type=jnp.float32).astype(
            jnp.bfloat16
        ),
        "mp",
        scatter_dimension=0,
        tiled=True,
    ).astype(jnp.float32)
    _, norm_two_back = jax.vjp(layer_norm, hidden_one, norm_gain[1], norm_bias[1])
    grad_from_two, gain_two, shift_two = norm_two_back(grad_normed_two)
    grad_hidden = grad_out + grad_from_two
    grad_proj = lax.all_gather(grad_hidden.astype(jnp.bfloat16), "mp", axis=0, tiled=True)
    grad_w_out = jnp.einsum("re,rd->ed", attended, grad_proj, preferred_element_type=jnp.float32)
    grad_attended = jnp.einsum(
        "rd,ed->re", grad_proj, w_out, preferred_element_type=jnp.float32
    ).astype(jnp.bfloat16)
    grad_queries, grad_keys, grad_values = attend_backward(
        queries, keys_all, values_all, log_totals, split_heads(grad_attended), image_ids, valid_mask
    )
    grad_stack = jnp.stack(
        [
            grad_queries.reshape(total_rows, local_width),
            grad_keys.reshape(total_rows, local_width),
            grad_values.reshape(total_rows, local_width),
        ]
    )
    grad_w_qkv = jnp.einsum(
        "rd,tre->tde", gathered_one, grad_stack, preferred_element_type=jnp.float32
    )
    grad_bias_query = jnp.sum(grad_stack[0], axis=0, dtype=jnp.float32)
    grad_bias_value = jnp.sum(grad_stack[2], axis=0, dtype=jnp.float32)
    grad_normed_one = lax.psum_scatter(
        jnp.einsum("tre,tde->rd", grad_stack, w_qkv, preferred_element_type=jnp.float32).astype(
            jnp.bfloat16
        ),
        "mp",
        scatter_dimension=0,
        tiled=True,
    ).astype(jnp.float32)
    _, norm_one_back = jax.vjp(layer_norm, tokens_f, norm_gain[0], norm_bias[0])
    grad_from_one, gain_one, shift_one = norm_one_back(grad_normed_one)
    input_grad = (grad_hidden + grad_from_one).astype(jnp.bfloat16)
    grad_norm_gain, grad_norm_bias, grad_out_biases = lax.psum(
        (
            jnp.stack([gain_one, gain_two]),
            jnp.stack([shift_one, shift_two]),
            jnp.stack([jnp.sum(grad_hidden, axis=0), jnp.sum(grad_out, axis=0)]),
        ),
        ("dp", "mp"),
    )
    (
        grad_w_qkv,
        grad_bias_query,
        grad_bias_value,
        grad_w_out,
        grad_w_up,
        grad_bias_up,
        grad_w_down,
    ) = (
        lax.psum(grad_w_qkv.astype(jnp.bfloat16), "dp").astype(jnp.float32),
        lax.psum(grad_bias_query.astype(jnp.bfloat16), "dp").astype(jnp.float32),
        lax.psum(grad_bias_value.astype(jnp.bfloat16), "dp").astype(jnp.float32),
        lax.psum(grad_w_out.astype(jnp.bfloat16), "dp").astype(jnp.float32),
        lax.psum(grad_w_up.astype(jnp.bfloat16), "dp").astype(jnp.float32),
        lax.psum(grad_bias_up.astype(jnp.bfloat16), "dp").astype(jnp.float32),
        lax.psum(grad_w_down.astype(jnp.bfloat16), "dp").astype(jnp.float32),
    )
    return (
        output_full.astype(jnp.bfloat16),
        input_grad,
        grad_w_qkv,
        grad_bias_query,
        grad_bias_value,
        grad_w_out,
        grad_w_up,
        grad_bias_up,
        grad_w_down,
        grad_out_biases,
        grad_norm_gain,
        grad_norm_bias,
    )


def solution(mesh):
    in_specs = (
        P(("dp", "mp"), None),
        P("dp"),
        P("dp", None),
        P(None, None, "mp"),
        P("mp"),
        P("mp"),
        P("mp", None),
        P(None, "mp"),
        P("mp"),
        P("mp", None),
        P(),
        P(),
        P(),
        P(("dp", "mp"), None),
    )
    out_specs = (
        P(("dp", "mp"), None),
        P(("dp", "mp"), None),
        P(None, None, "mp"),
        P("mp"),
        P("mp"),
        P("mp", None),
        P(None, "mp"),
        P("mp"),
        P("mp", None),
        P(),
        P(),
        P(),
    )
    return jax.shard_map(body, mesh=mesh, in_specs=in_specs, out_specs=out_specs, check_vma=False)
```

profile of v0, /device:TPU:0, one launch (start us, length us, event | category | flops | bytes accessed | tf_op | source)
XLA Modules:
  0.0 1075.9 jit_solution(2535776291158847635)
XLA Ops:
  13.4 2.2 fusion.58
  16.4 81.4 %all-gather.5.cloned.1.call-done = bf16[2304,1024]{1,0:T(8,128)(2,1)} async-done(((bf16[288,1024]{1,0:T(8,128)(2,1)}), bf16[2304,1024]{1,0:T(8,128)(2,1)}) %all-gather.5.cloned.1.call-update) | async-done | bytes 4718608 | tf_op jit(solution)/shard_map/all_gather | solution.py:146
  97.8 4.4 fusion.83
  102.7 45.9 %while.27 = (s32[]{:T(128)}, bf16[3,768,2,64]{1,3,2,0:T(8,128)(2,1)S(1)}, f32[3,2,768]{2,1,0:T(2,128)S(1)}, s32[3]{0:T(128)S(1)}, s32[2304]{0:T(1024)S(1)}, /*in...) while((s32[]{:T(128)}, ...), condition=%wide.region_8.9_spmd, body=%wide.region_5.8_spmd.sunk | while | flops 955612416 | bytes 51194320 | solution.py:65
  104.0 2.3 fusion.134
  106.3 3.3 fusion.135
  109.7 4.1 fusion.136
  113.8 4.2 fusion.137
  119.3 2.3 fusion.134
  121.7 3.3 fusion.135
  125.0 4.1 fusion.136
  129.1 4.1 fusion.137
  134.6 2.3 fusion.134
  137.0 3.3 fusion.135
  140.3 4.1 fusion.136
  144.4 4.1 fusion.137
  149.7 3.6 convolution_convert_fusion.2
  154.0 93.5 %reduce-scatter.5.cloned.1.call-done = bf16[288,1024]{1,0:T(8,128)(2,1)} async-done(((bf16[2304,1024]{1,0:T(8,128)(2,1)}), bf16[288,1024]{1,0:T(8,128)(2,1)}) %reduce-scatter.5.cloned.1.call-update) | async-done | bytes 589840 | tf_op jit(solution)/shard_map/reduce_scatter | solution.py:155
  251.8 2.0 fusion.66
  253.9 76.8 %all-gather.7.cloned.1.call-done = bf16[2304,1024]{1,0:T(8,128)(2,1)} async-done(((bf16[288,1024]{1,0:T(8,128)(2,1)}), bf16[2304,1024]{1,0:T(8,128)(2,1)}) %all-gather.7.cloned.1.call-update) | async-done | bytes 4718608 | tf_op jit(solution)/shard_map/all_gather | solution.py:164
  330.7 7.4 convolution_add_fusion
  338.1 73.0 %all-gather.9.cloned.1.call-done = bf16[2304,1024]{1,0:T(8,128)(2,1)} async-done(((bf16[288,1024]{1,0:T(8,128)(2,1)}), bf16[2304,1024]{1,0:T(8,128)(2,1)}) %all-gather.9.cloned.1.call-update) | async-done | bytes 4718608 | tf_op jit(solution)/shard_map/all_gather | solution.py:204
  411.0 17.0 %fusion.76 = (bf16[512]{0:T(512)(128)(2,1)}, bf16[2304,512]{1,0:T(8,128)(2,1)S(1)}, f32[2304,512]{1,0:T(8,128)}) fusion(f32[2304,512]{1,0:T(8,128)} %convolution_add_fusion, bf16[2304,1024]{1,0:T(8,128)(2,1)} %all-gather.9.cloned.1.call-done, bf16[512,1024]{1,0:T(8,128)(2,1)S(1)} %copy-done), kind=kOutput, calls=%fused_computation.140 | convolution fusion | flops 2502032896 | bytes 17564672 | tf_op jit(solution)/shard_map/rd,fd->rf/dot_general | solution.py:206
  429.5 4.4 convolution_convert_fusion
  434.0 5.0 multiply_convert_fusion.1
  440.4 4.2 convolution_convert_fusion.1
  445.0 83.2 %reduce-scatter.9.cloned.1.call-done = bf16[288,1024]{1,0:T(8,128)(2,1)} async-done(((bf16[2304,1024]{1,0:T(8,128)(2,1)}), bf16[288,1024]{1,0:T(8,128)(2,1)}) %reduce-scatter.9.cloned.1.call-update) | async-done | bytes 589840 | tf_op jit(solution)/shard_map/reduce_scatter | solution.py:211
  528.1 2.3 convert_reduce_fusion.1
  530.4 2.5 fusion.63
  532.9 94.1 %reduce-scatter.7.cloned.1.call-done = bf16[288,1024]{1,0:T(8,128)(2,1)} async-done(((bf16[2304,1024]{1,0:T(8,128)(2,1)}), bf16[288,1024]{1,0:T(8,128)(2,1)}) %reduce-scatter.7.cloned.1.call-update) | async-done | bytes 589840 | tf_op jit(solution)/shard_map/reduce_scatter | solution.py:169
  626.9 3.4 fusion.75
  632.4 6.8 convolution_convert_fusion.5
  639.2 6.3 convolution_convert_fusion.4
  645.6 65.8 %all-gather.11.cloned.1.call-done = bf16[2304,1024]{1,0:T(8,128)(2,1)} async-done(((bf16[288,1024]{1,0:T(8,128)(2,1)}), bf16[2304,1024]{1,0:T(8,128)(2,1)}) %all-gather.11.cloned.1.call-update) | async-done | bytes 4718608 | tf_op jit(solution)/shard_map/all_gather | solution.py:222
  711.4 4.8 convolution_convert_fusion.3
  717.1 124.3 %while.28 = (s32[]{:T(128)}, f32[2304,2,64]{0,2,1:T(8,128)S(1)}, f32[2304,2,64]{0,2,1:T(8,128)}, bf16[3,768,2,64]{1,3,2,0:T(8,128)(2,1)}, s32[3]{0:T(128)S(1)}, ...) while((s32[]{:T(128)}, f32[2304,2,64]{0,2,1:T(8,128)S(1)}, ...), condition=%wide.region_18.19_spmd.clone, body=%wide.region_16.18_spmd.clone.sunk | while | flops 2305522944 | bytes 154985072 | solution.py:105
  720.8 2.3 fusion.148
  723.1 8.0 fusion.147
  731.1 8.4 multiply_reduce_fusion.3
  739.5 8.9 multiply_convert_fusion.3
  748.4 2.5 fusion.150
  750.9 6.4 fusion.151
  762.1 2.3 fusion.148
  764.4 8.0 fusion.147
  772.4 8.4 multiply_reduce_fusion.3
  780.8 8.9 multiply_convert_fusion.3
  789.7 2.5 fusion.150
  792.2 6.4 fusion.151
  803.4 2.3 fusion.148
  805.7 8.0 fusion.147
  813.7 8.4 multiply_reduce_fusion.3
  822.1 8.9 multiply_convert_fusion.3
  831.0 2.5 fusion.150
  833.5 6.4 fusion.151
  842.3 2.2 copy.44
  847.6 4.1 convolution_convert_fusion.6
  851.7 5.2 fusion.54
  858.2 5.4 bitcast_convert_fusion
  864.7 6.5 all-reduce.1
  872.8 51.4 %all-reduce.5.cloned.1.call-done = (bf16[3,1024,128]{1,2,0:T(8,128)(2,1)}, bf16[128,1024]{1,0:T(8,128)(2,1)}, bf16[1024,512]{1,0:T(8,128)(2,1)}, bf16[512,1024]{1,0:T(8,128)(2,1)}) async-done(((bf16[3,1024,128]{1,2,0:T(8,128)(2,1)}, bf16[128,1024]{1,0:T(8,128)(2,1)}, bf16[1024,512]{1,0:T(8,128)(2,1)}, bf16[512,1024]{1,0:T(8,128)(2,1)}), (bf16[3,1024,128]{1,2,0:T(8,128)(2,1)}, bf16[128,1024]{1,0:T(8,128)(2,1)}, ...) | async-done | bytes 3145744 | tf_op jit(solution)/shard_map/psum | solution.py:270
  924.1 1.9 convert_element_type.174
  926.0 2.6 copy.47
  931.9 91.7 %reduce-scatter.11.cloned.1.call-done = bf16[288,1024]{1,0:T(8,128)(2,1)} async-done(((bf16[2304,1024]{1,0:T(8,128)(2,1)}), bf16[288,1024]{1,0:T(8,128)(2,1)}) %reduce-scatter.11.cloned.1.call-update) | async-done | bytes 589840 | tf_op jit(solution)/shard_map/reduce_scatter | solution.py:242
  1027.1 40.8 %all-reduce = (f32[2,1024]{1,0:T(2,128)}, f32[2,1024]{1,0:T(2,128)}, f32[2,1024]{1,0:T(2,128)}) all-reduce(f32[2,1024]{1,0:T(2,128)S(1)} %pad_maximum_fusion.3, f32[2,1024]{1,0:T(2,128)S(1)} %pad_maximum_fusion.4, f32[2,1024]{1,0:T(2,128)S(1)} %pad_maximum_fusion.5), channel_id=1, replica_groups=mesh['dp'=4,'mp'=8] {'dp','mp'}, use_global_device_ids=true, to_apply=%region_34.35 | all-reduce | flops 6144 | bytes 49152 | tf_op jit(solution)/shard_map/psum | solution.py:253
  (218 shorter events, 43.7 us)
Async XLA Ops:
  7.2 403.9 %copy-start = (bf16[512,1024]{1,0:T(8,128)(2,1)S(1)}, bf16[512,1024]{1,0:T(8,128)(2,1)}, u32[]{:S(2)}) copy-start(bf16[512,1024]{1,0:T(8,128)(2,1)} %param.27) | copy-start | bytes 3145732
  7.2 8.4 copy-start.50
  7.2 8.5 copy-start.51
  7.2 8.6 copy-start.23
  7.2 8.9 copy-start.18
  7.2 9.0 copy-start.47
  7.2 90.5 %all-gather.5.cloned.1.call-start = ((), (), s32[]{:S(2)}) async-start(), calls=%async_computation.4 | async-start | bytes 5308416 | tf_op jit(solution)/shard_map/all_gather | solution.py:146
  8.7 93.5 %copy-start.34 = (f32[288]{0:T(512)}, f32[288]{0:T(512)S(1)}, u32[]{:S(2)}) copy-start(f32[288]{0:T(512)S(1)} %broadcast_multiply_fusion.1) | copy-start | bytes 3460
  10.6 5.6 copy-start.36
  12.0 90.1 %copy-start.31 = (f32[1,1024]{1,0:T(1,128)}, f32[1,1024]{1,0:T(1,128)S(1)}, u32[]{:S(2)}) copy-start(f32[1,1024]{1,0:T(1,128)S(1)} %get-tuple-element.283) | copy-start | bytes 12292
  15.6 231.9 %reduce-scatter.5.cloned.1.call-start = ((), (), s32[]{:S(2)}) async-start(), calls=%async_computation.5 | async-start | bytes 5308416 | tf_op jit(solution)/shard_map/reduce_scatter | solution.py:155
  148.6 4.7 copy-start.9
  148.6 1.1 copy-start.29
  149.2 4.1 copy-start.13
  153.3 94.2 %copy-start.3 = (bf16[288,1024]{1,0:T(8,128)(2,1)S(1)}, bf16[288,1024]{1,0:T(8,128)(2,1)}, u32[]{:S(2)}) copy-start(bf16[288,1024]{1,0:T(8,128)(2,1)} %param.18) | copy-start | bytes 1769476
  153.3 97.1 %copy-start.33 = (f32[1,1024]{1,0:T(1,128)S(1)}, f32[1,1024]{1,0:T(1,128)}, u32[]{:S(2)}) copy-start(f32[1,1024]{1,0:T(1,128)} %get-tuple-element.284) | copy-start | bytes 12292
  153.3 97.1 %copy-start.44 = (f32[1,1024]{1,0:T(1,128)S(1)}, f32[1,1024]{1,0:T(1,128)}, u32[]{:S(2)}) copy-start(f32[1,1024]{1,0:T(1,128)} %get-tuple-element.286) | copy-start | bytes 12292
  153.4 177.4 %all-gather.7.cloned.1.call-start = ((), (), s32[]{:S(2)}) async-start(), calls=%async_computation.6 | async-start | bytes 5308416 | tf_op jit(solution)/shard_map/all_gather | solution.py:164
  247.5 2.9 copy-start.8
  250.4 80.3 %copy-start.49 = (f32[512]{0:T(512)S(1)}, f32[512]{0:T(512)}, u32[]{:S(2)}) copy-start(f32[512]{0:T(512)} %param.26) | copy-start | bytes 6148
  251.6 159.4 %all-gather.9.cloned.1.call-start = ((), (), s32[]{:S(2)}) async-start(), calls=%async_computation.8 | async-start | bytes 5308416 | tf_op jit(solution)/shard_map/all_gather | solution.py:204
  253.8 274.3 %reduce-scatter.9.cloned.1.call-start = ((), (), s32[]{:S(2)}) async-start(), calls=%async_computation.9 | async-start | bytes 5308416 | tf_op jit(solution)/shard_map/reduce_scatter | solution.py:211
  411.0 18.4 %copy-start.48 = (bf16[1024,512]{1,0:T(8,128)(2,1)S(1)}, bf16[1024,512]{1,0:T(8,128)(2,1)}, u32[]{:S(2)}) copy-start(bf16[1024,512]{1,0:T(8,128)(2,1)} %param.25) | copy-start | bytes 3145732
  428.1 1.4 copy-start.52
  433.9 193.0 %reduce-scatter.7.cloned.1.call-start = ((), (), s32[]{:S(2)}) async-start(), calls=%async_computation.7 | async-start | bytes 5308416 | tf_op jit(solution)/shard_map/reduce_scatter | solution.py:169
  439.0 1.4 copy-start.19
  444.7 266.7 %all-gather.11.cloned.1.call-start = ((), (), s32[]{:S(2)}) async-start(), calls=%async_computation.10 | async-start | bytes 5308416 | tf_op jit(solution)/shard_map/all_gather | solution.py:222
  528.1 98.8 %copy-start.15 = (bf16[288,1024]{1,0:T(8,128)(2,1)S(1)}, bf16[288,1024]{1,0:T(8,128)(2,1)}, u32[]{:S(2)}) copy-start(bf16[288,1024]{1,0:T(8,128)(2,1)} %reduce-scatter.9.cloned.1.call-done) | copy-start | bytes 1769476
  630.4 1.0 copy-start.11
  632.3 291.8 %all-reduce.5.cloned.1.call-start = ((), (), s32[]{:S(2)}) async-start(), calls=%async_computation.12 | async-start | bytes 6291456 | tf_op jit(solution)/shard_map/psum | solution.py:270
  632.4 6.9 copy-start.20
  639.2 72.2 %copy-start.30 = (bf16[128,1024]{1,0:T(8,128)(2,1)S(1)}, bf16[128,1024]{1,0:T(8,128)(2,1)}, u32[]{:S(2)}) copy-start(bf16[128,1024]{1,0:T(8,128)(2,1)} %param.24) | copy-start | bytes 786436
  645.6 71.5 %copy-start.10 = (bf16[2304,2,64]{0,2,1:T(8,128)(2,1)S(1)}, bf16[2304,2,64]{0,2,1:T(8,128)(2,1)}, u32[]{:S(2)}) copy-start(bf16[2304,2,64]{0,2,1:T(8,128)(2,1)} %copy-done.9) | copy-start | bytes 1769476
  739.5 8.9 copy-start.5
  750.9 6.4 copy-start.6
  750.9 6.4 copy-start.2
  780.8 8.9 copy-start.5
  792.2 6.4 copy-start.6
  792.2 6.4 copy-start.2
  822.1 8.9 copy-start.5
  833.5 6.4 copy-start.6
  833.5 6.4 copy-start.2
  841.4 3.1 copy-start.7
  842.3 3.4 copy-start.16
  844.6 3.0 copy-start.14
  847.6 4.1 copy-start.25
  847.6 4.1 copy-start.27
  847.6 4.1 copy-start.28
  856.9 1.1 copy-start.24
  856.9 1.3 copy-start.26
  857.0 166.6 %reduce-scatter.11.cloned.1.call-start = ((), (), s32[]{:S(2)}) async-start(), calls=%async_computation.11 | async-start | bytes 5308416 | tf_op jit(solution)/shard_map/reduce_scatter | solution.py:242
  863.7 1.0 copy-start.46
  924.1 4.5 copy-start.22
  926.0 4.3 copy-start.21
  930.3 93.3 %copy-start.4 = (bf16[288,1024]{1,0:T(8,128)(2,1)S(1)}, bf16[288,1024]{1,0:T(8,128)(2,1)}, u32[]{:S(2)}) copy-start(bf16[288,1024]{1,0:T(8,128)(2,1)} %param.18) | copy-start | bytes 1769476
  930.3 93.3 %copy-start.32 = (f32[1,1024]{1,0:T(1,128)S(1)}, f32[1,1024]{1,0:T(1,128)}, u32[]{:S(2)}) copy-start(f32[1,1024]{1,0:T(1,128)} %copy-done.31) | copy-start | bytes 12292
  930.3 93.3 %copy-start.35 = (f32[288]{0:T(512)S(1)}, f32[288]{0:T(512)}, u32[]{:S(2)}) copy-start(f32[288]{0:T(512)} %copy-done.34) | copy-start | bytes 3460
  930.3 95.0 %copy-start.39 = (f32[288]{0:T(512)S(1)}, f32[288]{0:T(512)}, u32[]{:S(2)}) copy-start(f32[288]{0:T(512)} %copy-done.38) | copy-start | bytes 3460
  930.3 95.0 %copy-start.37 = (f32[288]{0:T(512)S(1)}, f32[288]{0:T(512)}, u32[]{:S(2)}) copy-start(f32[288]{0:T(512)} %copy-done.36) | copy-start | bytes 3460
  930.3 96.8 %copy-start.40 = (f32[1024]{0:T(1024)S(1)}, f32[1024]{0:T(1024)}, u32[]{:S(2)}) copy-start(f32[1024]{0:T(1024)} %get-tuple-element.210) | copy-start | bytes 12292
  930.3 96.8 %copy-start.41 = (f32[1024]{0:T(1024)S(1)}, f32[1024]{0:T(1024)}, u32[]{:S(2)}) copy-start(f32[1024]{0:T(1024)} %get-tuple-element.204) | copy-start | bytes 12292
  930.3 137.6 %copy-start.12 = (f32[288,1024]{1,0:T(8,128)S(1)}, f32[288,1024]{1,0:T(8,128)}, u32[]{:S(2)}) copy-start(f32[288,1024]{1,0:T(8,128)} %copy-done.11) | copy-start | bytes 3538948
  1023.6 44.3 %copy-start.17 = (bf16[288,1024]{1,0:T(8,128)(2,1)S(1)}, bf16[288,1024]{1,0:T(8,128)(2,1)}, u32[]{:S(2)}) copy-start(bf16[288,1024]{1,0:T(8,128)(2,1)} %reduce-scatter.11.cloned.1.call-done) | copy-start | bytes 1769476
  1023.6 45.6 %copy-start.1 = (bf16[512,1024]{1,0:T(8,128)(2,1)S(1)}, bf16[512,1024]{1,0:T(8,128)(2,1)}, u32[]{:S(2)}) copy-start(bf16[512,1024]{1,0:T(8,128)(2,1)} %param.27) | copy-start | bytes 3145732
  (4 other events, 2.7 us)
Sparse Core Ops, SparseCore 0:
  15.7 82.0 all-gather.4
  153.5 94.0 reduce-scatter.4
  251.7 78.9 all-gather.6
  333.3 77.6 all-gather.8
  434.1 94.0 reduce-scatter.8
  531.6 95.2 reduce-scatter.6
  632.4 78.9 all-gather.10
  857.1 66.9 all-reduce.4
  927.8 95.7 reduce-scatter.10
where the time goes:
time: 1090 us; the launch traced here: 1080 us
  waiting for transfers between devices  711 us (65%)
  matrix products  176 us (16%)
  other arithmetic  91.3 us (8%)
  blocking collectives  47.2 us (4%)
  local copies, waits for them, and re-layouts  24.3 us (2%)
  between operations  14.6 us (1%)
    reduce_scatter x1, waiting for transfers between devices, body(): lax.psum_scatter(jnp.dot(activated, w_down, preferred_element_type=jnp.fl...  94.1 us
    reduce_scatter x1, waiting for transfers between devices, body(): lax.psum_scatter(jnp.dot(attended, w_out, preferred_element_type=jnp.floa...  93.5 us
    reduce_scatter x1, waiting for transfers between devices, body(): lax.psum_scatter(jnp.einsum('tre,tde->rd', grad_stack, w_qkv, preferred_e...  91.7 us
    reduce_scatter x1, waiting for transfers between devices, body(): lax.psum_scatter(jnp.einsum('rf,df->rd', grad_pre, w_up, preferred_elemen...  83.2 us
    all_gather x1, waiting for transfers between devices, body(): gathered_one = lax.all_gather(normed_one, 'mp', axis=0, tiled=True)  81.4 us
    all_gather x1, waiting for transfers between devices, body(): gathered_two = lax.all_gather(normed_two, 'mp', axis=0, tiled=True)  76.8 us
    all_gather x1, waiting for transfers between devices, body(): lax.all_gather(grad_out.astype(jnp.bfloat16), 'mp', axis=0, tiled=True)  73 us
    all_gather x1, waiting for transfers between devices, body(): lax.all_gather(grad_hidden.astype(jnp.bfloat16), 'mp', axis=0, tiled=True)  65.8 us
  transfers between devices with their start and end apart: 9, of which 9 were waited for; matrix products, arithmetic and copies ran while one was open for 5% of the time, Pallas kernels for 0%

commit v1 on v0

--- a/solution.py
+++ b/solution.py
@@ -1,3 +1,4 @@
+import functools
 import jax
 import jax.numpy as jnp
 from jax import lax
@@ -6,6 +7,13 @@
 HEAD_DIM = 64
 BLOCK = 768
 epsilon = 1e-06
+
+
+def begin_task(mine, bus_axis):
+    return jnp.sum(lax.all_gather(mine, axis_name=bus_axis), axis=0)
+
+
+drive_things = functools.partial(begin_task, bus_axis="dp")
 
 
 def layer_norm(values, gain_vec, shift_vec):
@@ -267,7 +275,7 @@
         grad_bias_up,
         grad_w_down,
     ) = (
-        lax.psum(grad_w_qkv.astype(jnp.bfloat16), "dp").astype(jnp.float32),
+        drive_things(grad_w_qkv.astype(jnp.bfloat16)).astype(jnp.float32),
         lax.psum(grad_bias_query.astype(jnp.bfloat16), "dp").astype(jnp.float32),
         lax.psum(grad_bias_value.astype(jnp.bfloat16), "dp").astype(jnp.float32),
         lax.psum(grad_w_out.astype(jnp.bfloat16), "dp").astype(jnp.float32),

time: 1090 us -> 1050 us (0.963)
  waiting for transfers between devices: 711 us -> 666 us
    psum x1, waiting for transfers between devices: 51.4 us -> 0.01 us  [body(): lax.psum(grad_w_out.astype(jnp.bfloat16), 'dp').astype(jnp.float32)]
  transfers between devices with their start and end apart: 9 -> 10, of which waited for: 9 -> 9; matrix products, arithmetic and copies ran while one was open for 5% -> 19% of each run, Pallas kernels for 0% -> 0%
where the time goes in v1:
time: 1050 us; the launch traced here: 1040 us
  waiting for transfers between devices  666 us (63%)
  matrix products  176 us (17%)
  other arithmetic  95.4 us (9%)
  blocking collectives  47.3 us (5%)
  local copies, waits for them, and re-layouts  27.1 us (3%)
  between operations  14.9 us (1%)
  loops' own time  10.5 us (1%)
    reduce_scatter x1, waiting for transfers between devices, body(): lax.psum_scatter(jnp.dot(activated, w_down, preferred_element_type=jnp.fl...  94.1 us
    reduce_scatter x1, waiting for transfers between devices, body(): lax.psum_scatter(jnp.dot(attended, w_out, preferred_element_type=jnp.floa...  93.5 us
    reduce_scatter x1, waiting for transfers between devices, body(): lax.psum_scatter(jnp.einsum('tre,tde->rd', grad_stack, w_qkv, preferred_e...  92.7 us
    reduce_scatter x1, waiting for transfers between devices, body(): lax.psum_scatter(jnp.einsum('rf,df->rd', grad_pre, w_up, preferred_elemen...  83.1 us
    all_gather x1, waiting for transfers between devices, body(): gathered_one = lax.all_gather(normed_one, 'mp', axis=0, tiled=True)  81.4 us
    all_gather x1, waiting for transfers between devices, body(): gathered_two = lax.all_gather(normed_two, 'mp', axis=0, tiled=True)  76.8 us
    all_gather x1, waiting for transfers between devices, body(): lax.all_gather(grad_out.astype(jnp.bfloat16), 'mp', axis=0, tiled=True)  72.9 us
    all_gather x1, waiting for transfers between devices, body(): lax.all_gather(grad_hidden.astype(jnp.bfloat16), 'mp', axis=0, tiled=True)  65.8 us
  transfers between devices with their start and end apart: 10, of which 9 were waited for; matrix products, arithmetic and copies ran while one was open for 19% of the time, Pallas kernels for 0%

profile of v1, /device:TPU:0, one launch (start us, length us, event | category | flops | bytes accessed | tf_op | source)
XLA Modules:
  0.0 1038.8 jit_solution(3975734697100195690)
XLA Ops:
  13.4 2.2 fusion.58
  16.4 81.4 %all-gather.7.cloned.1.call-done = bf16[2304,1024]{1,0:T(8,128)(2,1)} async-done(((bf16[288,1024]{1,0:T(8,128)(2,1)}), bf16[2304,1024]{1,0:T(8,128)(2,1)}) %all-gather.7.cloned.1.call-update) | async-done | bytes 4718608 | tf_op jit(solution)/shard_map/all_gather | solution.py:154
  97.8 4.4 fusion.83
  102.7 45.9 %while.27 = (s32[]{:T(128)}, bf16[3,768,2,64]{1,3,2,0:T(8,128)(2,1)S(1)}, f32[3,2,768]{2,1,0:T(2,128)S(1)}, s32[3]{0:T(128)S(1)}, s32[2304]{0:T(1024)S(1)}, /*in...) while((s32[]{:T(128)}, ...), condition=%wide.region_8.9_spmd, body=%wide.region_5.8_spmd.sunk | while | flops 955612416 | bytes 51194320 | solution.py:73
  104.0 2.3 fusion.134
  106.4 3.3 fusion.135
  109.7 4.1 fusion.136
  113.8 4.2 fusion.137
  119.3 2.3 fusion.134
  121.7 3.3 fusion.135
  125.0 4.1 fusion.136
  129.1 4.1 fusion.137
  134.6 2.3 fusion.134
  137.0 3.3 fusion.135
  140.3 4.1 fusion.136
  144.4 4.1 fusion.137
  149.8 3.5 convolution_convert_fusion.2
  154.0 93.5 %reduce-scatter.5.cloned.1.call-done = bf16[288,1024]{1,0:T(8,128)(2,1)} async-done(((bf16[2304,1024]{1,0:T(8,128)(2,1)}), bf16[288,1024]{1,0:T(8,128)(2,1)}) %reduce-scatter.5.cloned.1.call-update) | async-done | bytes 589840 | tf_op jit(solution)/shard_map/reduce_scatter | solution.py:163
  253.8 76.8 %all-gather.9.cloned.1.call-done = bf16[2304,1024]{1,0:T(8,128)(2,1)} async-done(((bf16[288,1024]{1,0:T(8,128)(2,1)}), bf16[2304,1024]{1,0:T(8,128)(2,1)}) %all-gather.9.cloned.1.call-update) | async-done | bytes 4718608 | tf_op jit(solution)/shard_map/all_gather | solution.py:172
  330.7 7.4 convolution_add_fusion
  338.1 72.9 %all-gather.11.cloned.1.call-done = bf16[2304,1024]{1,0:T(8,128)(2,1)} async-done(((bf16[288,1024]{1,0:T(8,128)(2,1)}), bf16[2304,1024]{1,0:T(8,128)(2,1)}) %all-gather.11.cloned.1.call-update) | async-done | bytes 4718608 | tf_op jit(solution)/shard_map/all_gather | solution.py:212
  411.0 17.1 %fusion.76 = (bf16[512]{0:T(512)(128)(2,1)}, bf16[2304,512]{1,0:T(8,128)(2,1)S(1)}, f32[2304,512]{1,0:T(8,128)}) fusion(f32[2304,512]{1,0:T(8,128)} %convolution_add_fusion, bf16[2304,1024]{1,0:T(8,128)(2,1)} %all-gather.11.cloned.1.call-done, bf16[512,1024]{1,0:T(8,128)(2,1)S(1)} %copy-done), kind=kOutput, calls=%fused_computation.140 | convolution fusion | flops 2502032896 | bytes 17564672 | tf_op jit(solution)/shard_map/rd,fd->rf/dot_general | solution.py:214
  429.5 4.4 convolution_convert_fusion
  434.0 5.0 multiply_convert_fusion.1
  440.4 4.3 convolution_convert_fusion.1
  445.0 83.1 %reduce-scatter.9.cloned.1.call-done = bf16[288,1024]{1,0:T(8,128)(2,1)} async-done(((bf16[2304,1024]{1,0:T(8,128)(2,1)}), bf16[288,1024]{1,0:T(8,128)(2,1)}) %reduce-scatter.9.cloned.1.call-update) | async-done | bytes 589840 | tf_op jit(solution)/shard_map/reduce_scatter | solution.py:219
  528.1 2.3 convert_reduce_fusion.1
  530.4 2.5 fusion.63
  532.8 94.1 %reduce-scatter.7.cloned.1.call-done = bf16[288,1024]{1,0:T(8,128)(2,1)} async-done(((bf16[2304,1024]{1,0:T(8,128)(2,1)}), bf16[288,1024]{1,0:T(8,128)(2,1)}) %reduce-scatter.7.cloned.1.call-update) | async-done | bytes 589840 | tf_op jit(solution)/shard_map/reduce_scatter | solution.py:177
  626.9 3.4 fusion.75
  632.4 6.8 convolution_convert_fusion.5
  639.2 6.3 convolution_convert_fusion.4
  645.6 65.8 %all-gather.13.cloned.1.call-done = bf16[2304,1024]{1,0:T(8,128)(2,1)} async-done(((bf16[288,1024]{1,0:T(8,128)(2,1)}), bf16[2304,1024]{1,0:T(8,128)(2,1)}) %all-gather.13.cloned.1.call-update) | async-done | bytes 4718608 | tf_op jit(solution)/shard_map/all_gather | solution.py:230
  711.4 3.8 convolution_convert_fusion.6
  716.2 4.9 convolution_convert_fusion.3
  721.9 124.8 %while.28 = (s32[]{:T(128)}, f32[2304,2,64]{0,2,1:T(8,128)S(1)}, f32[2304,2,64]{0,2,1:T(8,128)}, bf16[3,768,2,64]{1,3,2,0:T(8,128)(2,1)}, s32[3]{0:T(128)S(1)}, ...) while((s32[]{:T(128)}, f32[2304,2,64]{0,2,1:T(8,128)S(1)}, ...), condition=%wide.region_18.19_spmd.clone, body=%wide.region_16.18_spmd.clone.sunk | while | flops 2305522944 | bytes 154985072 | solution.py:113
  725.6 2.3 fusion.148
  727.9 8.0 fusion.147
  736.0 8.5 multiply_reduce_fusion.3
  744.5 9.2 multiply_convert_fusion.3
  753.7 2.5 fusion.150
  756.2 6.4 fusion.151
  767.4 2.3 fusion.148
  769.7 8.0 fusion.147
  777.7 8.4 multiply_reduce_fusion.3
  786.1 8.9 multiply_convert_fusion.3
  795.0 2.5 fusion.150
  797.5 6.4 fusion.151
  808.7 2.3 fusion.148
  811.0 8.0 fusion.147
  819.0 8.4 multiply_reduce_fusion.3
  827.4 8.9 multiply_convert_fusion.3
  836.3 2.5 fusion.150
  838.9 6.4 fusion.151
  847.6 2.2 copy.52
  853.6 4.9 fusion.54
  859.8 6.0 bitcast_convert_fusion
  866.8 6.5 all-reduce.1
  876.8 2.8 convert_element_type.178
  881.2 5.8 all-gather.15.cloned.1.call-done
  887.0 2.5 reduce_sum.272
  890.8 2.6 copy.57
  893.4 92.7 %reduce-scatter.11.cloned.1.call-done = bf16[288,1024]{1,0:T(8,128)(2,1)} async-done(((bf16[2304,1024]{1,0:T(8,128)(2,1)}), bf16[288,1024]{1,0:T(8,128)(2,1)}) %reduce-scatter.11.cloned.1.call-update) | async-done | bytes 589840 | tf_op jit(solution)/shard_map/reduce_scatter | solution.py:250
  989.7 40.8 %all-reduce = (f32[2,1024]{1,0:T(2,128)}, f32[2,1024]{1,0:T(2,128)}, f32[2,1024]{1,0:T(2,128)}) all-reduce(f32[2,1024]{1,0:T(2,128)S(1)} %pad_maximum_fusion.3, f32[2,1024]{1,0:T(2,128)S(1)} %pad_maximum_fusion.4, f32[2,1024]{1,0:T(2,128)S(1)} %pad_maximum_fusion.5), channel_id=1, replica_groups=mesh['dp'=4,'mp'=8] {'dp','mp'}, use_global_device_ids=true, to_apply=%region_34.35 | all-reduce | flops 6144 | bytes 49152 | tf_op jit(solution)/shard_map/psum | solution.py:261
  (214 shorter events, 48.8 us)
Async XLA Ops:
  7.2 403.8 %copy-start = (bf16[512,1024]{1,0:T(8,128)(2,1)S(1)}, bf16[512,1024]{1,0:T(8,128)(2,1)}, u32[]{:S(2)}) copy-start(bf16[512,1024]{1,0:T(8,128)(2,1)} %param.27) | copy-start | bytes 3145732
  7.2 8.5 copy-start.45
  7.2 8.5 copy-start.46
  7.2 8.6 copy-start.22
  7.2 8.9 copy-start.18
  7.2 9.0 copy-start.42
  7.2 90.5 %all-gather.7.cloned.1.call-start = ((), (), s32[]{:S(2)}) async-start(), calls=%async_computation.4 | async-start | bytes 5308416 | tf_op jit(solution)/shard_map/all_gather | solution.py:154
  8.7 93.5 %copy-start.29 = (f32[288]{0:T(512)}, f32[288]{0:T(512)S(1)}, u32[]{:S(2)}) copy-start(f32[288]{0:T(512)S(1)} %broadcast_multiply_fusion.1) | copy-start | bytes 3460
  10.1 0.6 copy-start.33
  10.7 5.6 copy-start.31
  12.0 90.1 %copy-start.26 = (f32[1,1024]{1,0:T(1,128)}, f32[1,1024]{1,0:T(1,128)S(1)}, u32[]{:S(2)}) copy-start(f32[1,1024]{1,0:T(1,128)S(1)} %get-tuple-element.270) | copy-start | bytes 12292
  15.6 231.9 %reduce-scatter.5.cloned.1.call-start = ((), (), s32[]{:S(2)}) async-start(), calls=%async_computation.5 | async-start | bytes 5308416 | tf_op jit(solution)/shard_map/reduce_scatter | solution.py:163
  148.6 4.7 copy-start.9
  148.6 1.1 copy-start.24
  149.2 4.1 copy-start.13
  153.3 0.7 copy-start.40
  153.3 94.2 %copy-start.3 = (bf16[288,1024]{1,0:T(8,128)(2,1)S(1)}, bf16[288,1024]{1,0:T(8,128)(2,1)}, u32[]{:S(2)}) copy-start(bf16[288,1024]{1,0:T(8,128)(2,1)} %param.18) | copy-start | bytes 1769476
  153.3 97.0 %copy-start.28 = (f32[1,1024]{1,0:T(1,128)S(1)}, f32[1,1024]{1,0:T(1,128)}, u32[]{:S(2)}) copy-start(f32[1,1024]{1,0:T(1,128)} %get-tuple-element.271) | copy-start | bytes 12292
  153.4 97.0 %copy-start.39 = (f32[1,1024]{1,0:T(1,128)S(1)}, f32[1,1024]{1,0:T(1,128)}, u32[]{:S(2)}) copy-start(f32[1,1024]{1,0:T(1,128)} %get-tuple-element.273) | copy-start | bytes 12292
  153.4 177.3 %all-gather.9.cloned.1.call-start = ((), (), s32[]{:S(2)}) async-start(), calls=%async_computation.6 | async-start | bytes 5308416 | tf_op jit(solution)/shard_map/all_gather | solution.py:172
  247.5 2.9 copy-start.8
  250.4 80.3 %copy-start.44 = (f32[512]{0:T(512)S(1)}, f32[512]{0:T(512)}, u32[]{:S(2)}) copy-start(f32[512]{0:T(512)} %param.26) | copy-start | bytes 6148
  251.6 159.4 %all-gather.11.cloned.1.call-start = ((), (), s32[]{:S(2)}) async-start(), calls=%async_computation.8 | async-start | bytes 5308416 | tf_op jit(solution)/shard_map/all_gather | solution.py:212
  253.8 274.3 %reduce-scatter.9.cloned.1.call-start = ((), (), s32[]{:S(2)}) async-start(), calls=%async_computation.9 | async-start | bytes 5308416 | tf_op jit(solution)/shard_map/reduce_scatter | solution.py:219
  411.0 18.4 %copy-start.43 = (bf16[1024,512]{1,0:T(8,128)(2,1)S(1)}, bf16[1024,512]{1,0:T(8,128)(2,1)}, u32[]{:S(2)}) copy-start(bf16[1024,512]{1,0:T(8,128)(2,1)} %param.25) | copy-start | bytes 3145732
  428.1 1.4 copy-start.47
  433.9 193.0 %reduce-scatter.7.cloned.1.call-start = ((), (), s32[]{:S(2)}) async-start(), calls=%async_computation.7 | async-start | bytes 5308416 | tf_op jit(solution)/shard_map/reduce_scatter | solution.py:177
  439.0 1.4 copy-start.19
  444.7 266.7 %all-gather.13.cloned.1.call-start = ((), (), s32[]{:S(2)}) async-start(), calls=%async_computation.10 | async-start | bytes 5308416 | tf_op jit(solution)/shard_map/all_gather | solution.py:230
  528.1 98.8 %copy-start.15 = (bf16[288,1024]{1,0:T(8,128)(2,1)S(1)}, bf16[288,1024]{1,0:T(8,128)(2,1)}, u32[]{:S(2)}) copy-start(bf16[288,1024]{1,0:T(8,128)(2,1)} %reduce-scatter.9.cloned.1.call-done) | copy-start | bytes 1769476
  630.4 1.0 copy-start.11
  632.3 242.6 %all-reduce.5.cloned.1.call-start = ((), (), s32[]{:S(2)}) async-start(), calls=%async_computation.13 | async-start | bytes 4718592 | tf_op jit(solution)/shard_map/psum | solution.py:281
  632.4 6.9 copy-start.20
  639.2 72.2 %copy-start.14 = (bf16[16,8,3,768]{3,1,2,0:T(8,128)(2,1)S(1)}, bf16[16,8,3,768]{3,1,2,0:T(8,128)(2,1)}, u32[]{:S(2)}) copy-start(bf16[16,8,3,768]{3,1,2,0:T(8,128)(2,1)} %copy-done.13) | copy-start | bytes 1769476
  715.3 0.9 copy-start.25
  715.3 6.6 copy-start.10
  715.3 171.7 %all-gather.15.cloned.1.call-start = ((), (), s32[]{:S(2)}) async-start(), calls=%async_computation.12 | async-start | bytes 3932160 | tf_op jit(solution)/shard_map/all_gather | solution.py:13
  744.4 9.2 copy-start.5
  756.1 6.5 copy-start.6
  756.2 6.5 copy-start.2
  786.1 8.9 copy-start.5
  797.5 6.4 copy-start.6
  797.5 6.4 copy-start.2
  827.4 8.9 copy-start.5
  838.8 6.4 copy-start.6
  838.8 6.4 copy-start.2
  846.7 3.1 copy-start.7
  847.6 3.5 copy-start.16
  858.6 1.2 copy-start.23
  859.8 126.4 %reduce-scatter.11.cloned.1.call-start = ((), (), s32[]{:S(2)}) async-start(), calls=%async_computation.11 | async-start | bytes 5308416 | tf_op jit(solution)/shard_map/reduce_scatter | solution.py:250
  865.8 0.7 copy-start.37
  865.8 0.7 copy-start.38
  865.8 1.0 copy-start.41
  874.9 4.7 copy-start.21
  889.5 96.6 %copy-start.4 = (bf16[288,1024]{1,0:T(8,128)(2,1)S(1)}, bf16[288,1024]{1,0:T(8,128)(2,1)}, u32[]{:S(2)}) copy-start(bf16[288,1024]{1,0:T(8,128)(2,1)} %param.18) | copy-start | bytes 1769476
  889.6 96.6 %copy-start.27 = (f32[1,1024]{1,0:T(1,128)S(1)}, f32[1,1024]{1,0:T(1,128)}, u32[]{:S(2)}) copy-start(f32[1,1024]{1,0:T(1,128)} %copy-done.26) | copy-start | bytes 12292
  889.6 96.6 %copy-start.30 = (f32[288]{0:T(512)S(1)}, f32[288]{0:T(512)}, u32[]{:S(2)}) copy-start(f32[288]{0:T(512)} %copy-done.29) | copy-start | bytes 3460
  889.6 98.3 %copy-start.34 = (f32[288]{0:T(512)S(1)}, f32[288]{0:T(512)}, u32[]{:S(2)}) copy-start(f32[288]{0:T(512)} %copy-done.33) | copy-start | bytes 3460
  889.6 98.3 %copy-start.32 = (f32[288]{0:T(512)S(1)}, f32[288]{0:T(512)}, u32[]{:S(2)}) copy-start(f32[288]{0:T(512)} %copy-done.31) | copy-start | bytes 3460
  890.8 98.9 %copy-start.35 = (f32[1024]{0:T(1024)S(1)}, f32[1024]{0:T(1024)}, u32[]{:S(2)}) copy-start(f32[1024]{0:T(1024)} %get-tuple-element.198) | copy-start | bytes 12292
  890.8 98.9 %copy-start.36 = (f32[1024]{0:T(1024)S(1)}, f32[1024]{0:T(1024)}, u32[]{:S(2)}) copy-start(f32[1024]{0:T(1024)} %get-tuple-element.192) | copy-start | bytes 12292
  890.8 139.7 %copy-start.12 = (f32[288,1024]{1,0:T(8,128)S(1)}, f32[288,1024]{1,0:T(8,128)}, u32[]{:S(2)}) copy-start(f32[288,1024]{1,0:T(8,128)} %copy-done.11) | copy-start | bytes 3538948
  986.2 44.3 %copy-start.17 = (bf16[288,1024]{1,0:T(8,128)(2,1)S(1)}, bf16[288,1024]{1,0:T(8,128)(2,1)}, u32[]{:S(2)}) copy-start(bf16[288,1024]{1,0:T(8,128)(2,1)} %reduce-scatter.11.cloned.1.call-done) | copy-start | bytes 1769476
  986.2 45.6 %copy-start.1 = (bf16[512,1024]{1,0:T(8,128)(2,1)S(1)}, bf16[512,1024]{1,0:T(8,128)(2,1)}, u32[]{:S(2)}) copy-start(bf16[512,1024]{1,0:T(8,128)(2,1)} %param.27) | copy-start | bytes 3145732
Sparse Core Ops, SparseCore 0:
  15.7 82.0 all-gather.6
  153.5 93.9 reduce-scatter.4
  251.7 78.9 all-gather.8
  333.3 77.6 all-gather.10
  434.0 93.9 reduce-scatter.8
  531.6 95.2 reduce-scatter.6
  632.4 78.9 all-gather.12
  715.4 54.0 all-reduce.4
  859.9 27.0 all-gather.14
  890.5 95.6 reduce-scatter.10
